TPU v7x, 32 devices: a whole 2x2x4 slice. The times are simulated.
32 devices in a mesh: groups: 2 (over y), row: 4 (over z), head: 4 (over x, core).
Axes of the slice: x: 2, y: 2, z: 4, core: 2. Of those that a mesh axis runs over, the one named last changes fastest.
Arguments:
- tokens: bfloat16 [32, 2048], P('groups'), parts along dimension 0, may hold values from -6 to 6
- query_weight: bfloat16 [2048, 3072], P('row', 'head'), may hold values from -0.125 to 0.125
- latent_weight: bfloat16 [512, 4096], P('row', 'head'), may hold values from -0.25 to 0.25
- output_weight: bfloat16 [2048, 2048], P('row', 'head'), may hold values from -0.5 to 0.5
- cache_latent: bfloat16 [32, 2048, 512], P(('groups', 'row'), 'head'), parts along dimension 0, may hold values from -32 to 32
- cache_rope: bfloat16 [32, 64, 2048], P(('groups', 'row'), None, 'head'), parts along dimension 0, may hold values from -1800 to 1800
- lengths: int32 [32], P('groups'), parts along dimension 0, may hold values from 1 to 2048
- slot_seq: int32 [32], P('groups'), parts along dimension 0, may hold values from 0 to 15, each once
Outputs:
- attn_out: bfloat16 [32, 2048], P(('groups', 'row'), 'head'), parts along dimension 0
There are 2 independent parts, one for each index of `groups`. A program takes and returns all parts, laid end to end along the dimension named above; an argument that names none is the same for every part. Nothing has to cross between parts.
Inputs may be any that keep to these rules, and one draw needn't show every extreme that they name: Cache row i belongs to sequence slot_seq[i], and output row i is that sequence's. Positions at or past lengths[s] of a sequence hold stale entries that are not read; its new token stands at position lengths[s] - 1.
All inputs are finite; a program needn't handle non-finite values.
Results may differ from a plain program's by a relative error of at most 0.039.
Values may be sent and summed in bfloat16 or wider, within the bound.
A program may use at most 64 MiB of HBM per device.

v0:
```python
import jax
import jax.numpy as jnp
from jax import lax
from jax.sharding import PartitionSpec as P

D = 2048
H = 16
NOPE = 128
ROPE = 64
V = 128
LAT = 512
BLOCK = 256


neg_big = -1e30


def combined_all(part, axis, combine):
    gathered = jax.tree.map(lambda a: lax.all_gather(a, axis), part)

    def take(source):
        return jax.tree.map(lambda a: lax.dynamic_index_in_dim(a, source, 0, False), gathered)

    return lax.fori_loop(
        1, lax.axis_size(axis), lambda source, state: combine(state, take(source)), take(0)
    )


def absorb(query_weight, output_weight, kv_heads):
    width = query_weight.shape[0]
    head_total = kv_heads.shape[1]
    query_heads = query_weight.reshape(width, head_total, NOPE + ROPE)
    out_heads = output_weight.reshape(width, head_total, V)
    nope_part = jnp.einsum(
        "dhn,lhn->dhl",
        query_heads[:, :, :NOPE],
        kv_heads[:, :, :NOPE],
        preferred_element_type=jnp.float32,
    ).astype(jnp.bfloat16)
    query_abs = jnp.concatenate([nope_part, query_heads[:, :, NOPE:]], axis=2).reshape(width, -1)
    out_abs = jnp.einsum(
        "dhv,lhv->dhl", out_heads, kv_heads[:, :, NOPE:], preferred_element_type=jnp.float32
    ).astype(jnp.bfloat16)
    return (query_abs, out_abs.reshape(width, -1))


def rotate(queries, seq_len):
    half_width = ROPE // 2
    inverse_freq = jnp.power(10000.0, -2.0 * jnp.arange(half_width, dtype=jnp.float32) / ROPE)
    angles = (seq_len - 1).astype(jnp.float32)[:, None] * inverse_freq[None, :]
    cosine = jnp.cos(angles)[:, None, :]
    sine = jnp.sin(angles)[:, None, :]
    first_half = queries[:, :, LAT : LAT + half_width]
    second_half = queries[:, :, LAT + half_width :]
    rotated = jnp.concatenate(
        [first_half * cosine - second_half * sine, first_half * sine + second_half * cosine], axis=2
    )
    return jnp.concatenate([queries[:, :, :LAT], rotated], axis=2)


def combine(earlier, later):
    earlier_max, earlier_sum, earlier_acc = earlier
    later_max, later_sum, later_acc = later
    peak_max = jnp.maximum(earlier_max, later_max)
    earlier_scale = jnp.exp(earlier_max - peak_max)
    later_scale = jnp.exp(later_max - peak_max)
    summed = earlier_sum * earlier_scale + later_sum * later_scale
    weighted = earlier_acc * earlier_scale[..., None] + later_acc * later_scale[..., None]
    return (peak_max, summed, weighted)


def local(
    tokens, query_weight, latent_weight, output_weight, cache_latent, cache_rope, lengths, slot_seq
):
    heads_dev = query_weight.shape[1] // (NOPE + ROPE)
    seq_dev = cache_latent.shape[0]
    seg_len = cache_latent.shape[1]
    latent_full = lax.all_gather(latent_weight, "row", axis=0, tiled=True)
    kv_heads = latent_full.reshape(LAT, heads_dev, NOPE + V)
    full_query, full_out = (
        lax.all_gather(query_weight, "row", axis=0, tiled=True),
        lax.all_gather(output_weight, "row", axis=0, tiled=True),
    )
    query_abs, out_abs = absorb(full_query, full_out, kv_heads)
    first_row = lax.axis_index("row") * seq_dev
    seq_ids = lax.dynamic_slice_in_dim(slot_seq, first_row, seq_dev)
    chosen = tokens[seq_ids]
    seq_len = lengths[seq_ids]
    queries = jnp.dot(chosen, query_abs, preferred_element_type=jnp.float32).reshape(
        seq_dev, heads_dev, LAT + ROPE
    )
    queries = (
        rotate(queries, seq_len).astype(jnp.bfloat16).reshape(seq_dev, heads_dev * (LAT + ROPE))
    )
    queries = lax.all_gather(queries, "head", axis=1, tiled=True).reshape(seq_dev, H, LAT + ROPE)
    query_latent = queries[:, :, :LAT]
    query_rope = queries[:, :, LAT:]
    score_scale = 1.0 / jnp.sqrt(jnp.float32(NOPE + ROPE))
    offset = lax.axis_index("head") * seg_len
    local_len = jnp.clip(seq_len - offset, 0, seg_len)
    live_blocks = (jnp.max(local_len) + BLOCK - 1) // BLOCK

    def advance(block_idx, running):
        run_max, run_sum, run_acc = running
        begin_at = block_idx * BLOCK
        latent_blk = lax.dynamic_slice_in_dim(cache_latent, begin_at, BLOCK, 1)
        rope_blk = lax.dynamic_slice_in_dim(cache_rope, begin_at, BLOCK, 2)
        scores = jnp.einsum(
            "bhl,btl->bht", query_latent, latent_blk, preferred_element_type=jnp.float32
        )
        scores = (
            scores
            + jnp.einsum("bhr,brt->bht", query_rope, rope_blk, preferred_element_type=jnp.float32)
        ) * score_scale
        in_range = (begin_at + jnp.arange(BLOCK, dtype=jnp.int32))[None, None, :] < local_len[
            :, None, None
        ]
        masked = jnp.where(in_range, scores, neg_big)
        new_max = jnp.maximum(run_max, jnp.max(masked, axis=2))
        weights = jnp.where(in_range, jnp.exp(masked - new_max[..., None]), 0.0)
        factor = jnp.exp(run_max - new_max)
        run_sum = run_sum * factor + jnp.sum(weights, axis=2)
        run_acc = run_acc * factor[..., None] + jnp.einsum(
            "bht,btl->bhl",
            weights.astype(jnp.bfloat16),
            latent_blk,
            preferred_element_type=jnp.float32,
        )
        return (new_max, run_sum, run_acc)

    initial = (
        jnp.full((seq_dev, H), neg_big, jnp.float32),
        jnp.zeros((seq_dev, H), jnp.float32),
        jnp.zeros((seq_dev, H, LAT), jnp.float32),
    )
    partial_state = lax.fori_loop(0, live_blocks, advance, initial)
    merged_max, merged_sum, merged_acc = combined_all(partial_state, "head", combine)
    latent_out = (merged_acc / merged_sum[..., None]).astype(jnp.bfloat16)
    own_heads = lax.dynamic_slice_in_dim(
        latent_out, lax.axis_index("head") * heads_dev, heads_dev, 1
    )
    out_term = jnp.einsum(
        "bhl,dhl->bd",
        own_heads,
        out_abs.reshape(D, heads_dev, LAT),
        preferred_element_type=jnp.float32,
    )
    return lax.psum_scatter(out_term, "head", scatter_dimension=1, tiled=True).astype(jnp.bfloat16)


def solution(mesh):
    placed = (
        P("groups", None),
        P("row", "head"),
        P("row", "head"),
        P("row", "head"),
        P(("groups", "row"), "head", None),
        P(("groups", "row"), None, "head"),
        P("groups"),
        P("groups"),
    )
    return jax.shard_map(
        local, mesh=mesh, in_specs=placed, out_specs=P(("groups", "row"), "head"), check_vma=False
    )
```

profile of v0, /device:TPU:0, one launch (start us, length us, event | category | flops | bytes accessed | tf_op | source)
XLA Modules:
  0.0 190.2 jit_solution(7725425204575464518)
XLA Ops:
  6.5 2.3 %copy.30 = bf16[512,768]{0,1:T(8,128)(2,1)} copy(bf16[512,768]{1,0:T(8,128)(2,1)} %param.13) | data formatting | bytes 1572864 | tf_op args[1]
  8.9 0.0 all-gather.11.cloned.1.call-update
  8.9 0.0 all-gather.9.cloned.1.call-start
  9.0 1.8 copy.28
  10.8 0.0 all-gather.9.cloned.1.call-update
  10.8 0.0 all-gather.13.cloned.1.call-start
  10.8 2.0 %copy.36 = bf16[512,512]{0,1:T(8,128)(2,1)} copy(bf16[512,512]{1,0:T(8,128)(2,1)} %param.15) | data formatting | bytes 1048576 | tf_op args[3]
  12.9 0.0 all-gather.13.cloned.1.call-update
  12.9 0.0 reduce-scatter.4.cloned.1.call-start
  13.0 0.7 compare_select_fusion
  13.7 1.3 gather_fusion
  15.0 0.6 fusion.42
  16.3 0.6 gather_fusion.1
  16.9 0.1 multiply_cosine_fusion
  17.0 58.2 %all-gather.11.cloned.1.call-done = bf16[2048,768]{0,1:T(8,128)(2,1)} async-done(((bf16[512,768]{0,1:T(8,128)(2,1)}), bf16[2048,768]{0,1:T(8,128)(2,1)}) %all-gather.11.cloned.1.call-update) | async-done | bytes 3145744 | tf_op jit(solution)/shard_map/all_gather | solution.py:81
  75.2 2.3 %slice.51 = bf16[2048,4,64]{0,2,1:T(8,128)(2,1)} slice(bf16[2048,4,192]{0,2,1:T(8,128)(2,1)} %bitcast.61), slice={[0:2048], [0:4], [128:192]} | slice | bytes 2097152 | tf_op jit(solution)/shard_map/slice | solution.py:40
  77.5 27.8 %all-gather.9.cloned.1.call-done = bf16[512,1024]{0,1:T(8,128)(2,1)} async-done(((bf16[128,1024]{0,1:T(8,128)(2,1)}), bf16[512,1024]{0,1:T(8,128)(2,1)}) %all-gather.9.cloned.1.call-update) | async-done | bytes 1048592 | tf_op jit(solution)/shard_map/all_gather | solution.py:78
  105.4 4.2 %convert_bitcast_fusion = bf16[2048,4,512]{0,2,1:T(8,128)(2,1)S(1)} fusion(bf16[2048,4,192]{0,2,1:T(8,128)(2,1)} %bitcast.62, bf16[512,4,256]{0,2,1:T(8,128)(2,1)} %bitcast.64), kind=kOutput, calls=%fused_computation.40 | convolution fusion | flops 1077936128 | bytes 11010048 | tf_op jit(solution)/shard_map/dhn,lhn->dhl/dot_general | solution.py:34
  109.6 2.8 %fusion.20 = f32[4,4,576]{2,0,1:T(4,128)S(1)} fusion(bf16[2048,4,64]{0,2,1:T(8,128)(2,1)S(1)} %copy-done.3, bf16[2048,4,512]{0,2,1:T(8,128)(2,1)S(1)} %convert_bitcast_fusion, bf16[4,2048]{1,0:T(4,128)(2,1)S(1)} %gather_fusion.1), kind=kOutput, calls=%fused_computation.34 | convolution fusion | flops 56623104 | bytes 9490432 | tf_op jit(solution)/shard_map/dot_general | solution.py:89
  112.5 0.1 subtract_convert_fusion
  112.5 0.1 pad_maximum_fusion
  112.6 0.1 convert_element_type.36
  112.7 5.3 %all_gather.32 = bf16[4,9216]{1,0:T(4,128)(2,1)S(1)} all-gather(bf16[4,2304]{1,0:T(4,128)(2,1)S(1)} %convert_element_type.36), channel_id=1, replica_groups=mesh['groups'=2,'row'=4,'head'=4] {'head'}, dimensions={1}, use_global_device_ids=true | all-gather | bytes 92160 | tf_op jit(solution)/shard_map/all_gather | solution.py:95
  118.0 0.1 reshape.117
  118.2 2.4 %while.33 = (s32[]{:T(128)}, f32[4,16]{1,0:T(4,128)S(1)}, f32[4,16]{1,0:T(4,128)S(1)}, f32[4,16,512]{2,1,0:T(8,128)S(1)}, s32[]{:T(128)}, /*index=5*/s32[4]{0:T(...) while((s32[]{:T(128)}, f32[4,16]{1,0:T(4,128)S(1)}, ...), condition=%wide.region_4.5_spmd, body=%wide.region_1.4_spmd.sunk | while | flops 35882372 | bytes 2914003 | solution.py:136
  118.2 0.4 fusion.62
  118.6 0.1 broadcast_compare_fusion.2
  118.7 0.2 fusion.63
  119.0 0.2 fusion.64
  119.1 0.3 convolution_add_fusion.3
  119.5 0.4 fusion.62
  119.8 0.1 broadcast_compare_fusion.2
  119.9 0.2 fusion.63
  120.2 0.2 fusion.64
  120.3 0.3 convolution_add_fusion.3
  120.6 7.3 %all-gather.2 = f32[16,16,512]{2,1,0:T(8,128)S(1)} all-gather(f32[4,16,512]{2,1,0:T(8,128)S(1)} %get-tuple-element.239), channel_id=4, replica_groups=mesh['groups'=2,'row'=4,'head'=4] {'head'}, dimensions={0}, use_global_device_ids=true | all-gather | bytes 655360 | tf_op jit(solution)/shard_map/all_gather | solution.py:19
  127.9 5.2 %all-gather.4 = f32[4,4,16]{2,1,0:T(4,128)S(1)} all-gather(f32[1,4,16]{2,1,0:T(4,128)S(1)} %bitcast.68), channel_id=3, replica_groups=mesh['groups'=2,'row'=4,'head'=4] {'head'}, dimensions={0}, use_global_device_ids=true | all-gather | bytes 1280 | tf_op jit(solution)/shard_map/all_gather | solution.py:19
  133.1 5.2 %all-gather.3 = f32[4,4,16]{2,1,0:T(4,128)S(1)} all-gather(f32[1,4,16]{2,1,0:T(4,128)S(1)} %bitcast.66), channel_id=2, replica_groups=mesh['groups'=2,'row'=4,'head'=4] {'head'}, dimensions={0}, use_global_device_ids=true | all-gather | bytes 1280 | tf_op jit(solution)/shard_map/all_gather | solution.py:19
  138.3 0.4 while.34
  138.3 0.1 fusion.66
  138.5 0.1 fusion.66
  138.6 0.1 fusion.66
  138.7 0.1 copy.34
  138.8 0.1 copy.33
  138.9 12.0 %all-gather.13.cloned.1.call-done = bf16[2048,512]{0,1:T(8,128)(2,1)} async-done(((bf16[512,512]{0,1:T(8,128)(2,1)}), bf16[2048,512]{0,1:T(8,128)(2,1)}) %all-gather.13.cloned.1.call-update) | async-done | bytes 2097168 | tf_op jit(solution)/shard_map/all_gather | solution.py:82
  151.0 7.3 %fusion.28 = f32[2048,4]{1,0:T(8,128)} fusion(bf16[2048,4,128]{0,2,1:T(8,128)(2,1)} %bitcast.69, bf16[512,4,256]{0,2,1:T(8,128)(2,1)} %bitcast.65, f32[4,16,512]{2,0,1:T(4,128)S(1)} %copy.34, s32[]{:T(128)S(6)} %select_n.49, f32[4,4]{0,1:T(4,128)S(1)} %constant_dynamic-slice_fusion), kind=kOutput, calls=%fused_computation.42 | convolution fusion | flops 1111506944 | bytes 2689028 | tf_op jit(solution)/shard_map/bhl,dhl->bd/dot_general | solution.py:142
  158.3 23.7 %reduce-scatter.4.cloned.1.call-done = f32[512,4]{1,0:T(8,128)} async-done(((f32[2048,4]{1,0:T(8,128)}), f32[512,4]{1,0:T(8,128)}) %reduce-scatter.4.cloned.1.call-update) | async-done | bytes 8208
  182.0 1.7 copy.42
  (34 shorter events, 0.3 us)
Async XLA Ops:
  6.5 9.8 %copy-start = (bf16[16,2048]{1,0:T(8,128)(2,1)S(1)}, bf16[16,2048]{1,0:T(8,128)(2,1)}, u32[]{:S(2)}) copy-start(bf16[16,2048]{1,0:T(8,128)(2,1)} %param.12) | copy-start | bytes 196612
  6.5 68.7 %all-gather.11.cloned.1.call-start = ((), (), s32[]{:S(2)}) async-start(), calls=%async_computation.2 | async-start | bytes 3932160 | tf_op jit(solution)/shard_map/all_gather | solution.py:81
  8.9 96.5 %all-gather.9.cloned.1.call-start = ((), (), s32[]{:S(2)}) async-start(), calls=%async_computation.1 | async-start | bytes 1310720 | tf_op jit(solution)/shard_map/all_gather | solution.py:78
  10.8 140.2 %all-gather.13.cloned.1.call-start = ((), (), s32[]{:S(2)}) async-start(), calls=%async_computation.3 | async-start | bytes 2621440 | tf_op jit(solution)/shard_map/all_gather | solution.py:82
  12.9 169.1 %reduce-scatter.4.cloned.1.call-start = ((), (), s32[]{:S(2)}) async-start(), calls=%async_computation.4 | async-start | bytes 1310720
  105.4 4.2 %copy-start.3 = (bf16[2048,4,64]{0,2,1:T(8,128)(2,1)S(1)}, bf16[2048,4,64]{0,2,1:T(8,128)(2,1)}, u32[]{:S(2)}) copy-start(bf16[2048,4,64]{0,2,1:T(8,128)(2,1)} %slice.51) | copy-start | bytes 3145732
  109.6 8.6 %copy-start.1 = (bf16[4,512,512]{2,1,0:T(8,128)(2,1)S(1)}, bf16[4,512,512]{2,1,0:T(8,128)(2,1)}, u32[]{:S(2)}) copy-start(bf16[4,512,512]{2,1,0:T(8,128)(2,1)} %param.16) | copy-start | bytes 6291460
  109.6 8.6 %copy-start.2 = (bf16[4,64,512]{2,1,0:T(8,128)(2,1)S(1)}, bf16[4,64,512]{2,1,0:T(8,128)(2,1)}, u32[]{:S(2)}) copy-start(bf16[4,64,512]{2,1,0:T(8,128)(2,1)} %param.17) | copy-start | bytes 786436
Sparse Core Ops, SparseCore 0:
  9.0 66.1 all-gather.10
  76.8 28.5 all-gather.8
  107.0 43.9 all-gather.12
  158.4 23.5 reduce-scatter.3
where the time goes:
time: 191 us; the launch traced here: 190 us
  waiting for transfers between devices  122 us (64%)
  blocking collectives  22.9 us (12%)
  matrix products  16.1 us (8%)
  between operations  14 us (7%)
  local copies, waits for them, and re-layouts  12.5 us (7%)
  other arithmetic  2.54 us (1%)
    all_gather x1, waiting for transfers between devices, local(): lax.all_gather(query_weight, 'row', axis=0, tiled=True)  58.2 us
    all_gather x1, waiting for transfers between devices, local(): latent_full = lax.all_gather(latent_weight, 'row', axis=0, tiled=True)  27.8 us
    unnamed x5, waiting for transfers between devices  23.8 us
    all_gather x3, blocking collectives, combined_all(): gathered = jax.tree.map(lambda a: lax.all_gather(a, axis), part)  17.6 us
    all_gather x1, waiting for transfers between devices, local(): lax.all_gather(output_weight, 'row', axis=0, tiled=True)  12 us
    unnamed x12, local copies, waits for them, and re-layouts  7.88 us
    dot_general x1, matrix products, local(): jnp.einsum('bhl,dhl->bd', own_heads, out_abs.reshape(D, heads_dev, LAT),...  7.3 us
    all_gather x1, blocking collectives, local(): lax.all_gather(queries, 'head', axis=1, tiled=True)  5.26 us
  transfers between devices with their start and end apart: 4, of which 4 were waited for; matrix products, arithmetic and copies ran while one was open for 10% of the time, Pallas kernels for 0%

commit v1 on v0

--- a/solution.py
+++ b/solution.py
@@ -1,6 +1,11 @@
+import functools
+
 import jax
 import jax.numpy as jnp
+import numpy as np
 from jax import lax
+from jax.experimental import pallas as pl
+from jax.experimental.pallas import tpu as pltpu
 from jax.sharding import PartitionSpec as P
 
 D = 2048
@@ -148,6 +153,332 @@
     return lax.psum_scatter(out_term, "head", scatter_dimension=1, tiled=True).astype(jnp.bfloat16)
 
 
+F32 = jnp.float32
+BF16 = jnp.bfloat16
+MESH = pl.DeviceIdType.MESH
+
+
+def dot_nn(a, b):
+    return lax.dot_general(a, b, (((1,), (0,)), ((), ())), preferred_element_type=F32)
+
+
+def dot_nt(a, b):
+    return lax.dot_general(a, b, (((1,), (1,)), ((), ())), preferred_element_type=F32)
+
+
+def iota(shape, axis):
+    return lax.broadcasted_iota(jnp.int32, shape, axis)
+
+
+def fused(
+    nr, nh, sd, hd,
+    freq_h, tok_h, wq_h, wl_h, wo_h, cl_h, cr_h, len_h, slot_h,
+    out_ref,
+    freq, tok, wq, wl, wo, cl, cr, lens, slot,
+    a_send, a_recv, ar_send, ar_recv,
+    b_send, b_recv, br_send, br_recv,
+    st_send, st_recv, d_send, d_recv,
+    e_send, e_recv, f_send, f_recv,
+    load_sem,
+    a_ss, a_rs, ar_ss, ar_rs, b_ss, b_rs, br_ss, br_rs,
+    st_ss, st_rs, d_ss, d_rs, e_ss, e_rs, f_ss, f_rs,
+):
+    r = lax.axis_index("row")
+    h = lax.axis_index("head")
+    batch = nr * sd
+    rows = sd * hd
+    db = wq.shape[0]
+    seg = cl.shape[1]
+    lb = LAT // nr
+
+    def load(k, src, dst):
+        c = pltpu.make_async_copy(src, dst, load_sem.at[k])
+        c.start()
+        return c
+
+    ld_slot = load(0, slot_h, slot)
+    ld_len = load(1, len_h, lens)
+    ld_tok = load(2, tok_h.at[:, pl.ds(pl.multiple_of(r * db, 128), db)], tok)
+    ld_wq = load(3, wq_h, wq)
+    ld_freq = load(4, freq_h, freq)
+    ld_wl = load(5, wl_h, wl)
+    ld_cl = load(6, cl_h, cl)
+    ld_cr = load(7, cr_h, cr)
+    ld_wo = load(8, wo_h, wo)
+
+    order = [dr for dr in range(nr) if dr] + [0]
+    pairs = [(dr, dh) for dr in order for dh in range(nh) if dr or dh]
+    barrier = pltpu.get_barrier_semaphore()
+    for dr, dh in pairs:
+        pl.semaphore_signal(
+            barrier, inc=1,
+            device_id={"row": lax.rem(r + dr, nr), "head": lax.rem(h + dh, nh)},
+            device_id_type=MESH,
+        )
+    pending = []
+
+    def send(src, dst, ss, rs, dr, dh):
+        c = pltpu.make_async_remote_copy(
+            src_ref=src, dst_ref=dst, send_sem=ss, recv_sem=rs,
+            device_id={"row": lax.rem(r + dr, nr), "head": lax.rem(h + dh, nh)},
+            device_id_type=MESH,
+        )
+        c.start()
+        pending.append(c)
+        return c
+
+    ld_slot.wait()
+    ld_len.wait()
+    ld_tok.wait()
+    pick_row = iota((batch, batch), 0)
+    picked = jnp.zeros((batch, batch), jnp.int32)
+    for i in range(batch):
+        picked = jnp.where(pick_row == i, slot[i], picked)
+    pick = (iota((batch, batch), 1) == picked).astype(F32).astype(BF16)
+    chosen = dot_nn(pick, tok[...]).astype(BF16)
+    ld_wq.wait()
+    part = dot_nn(chosen, wq[...])
+    width = NOPE + ROPE
+    nope = jnp.concatenate([part[:, width * j : width * j + NOPE] for j in range(hd)], axis=1)
+    rope = jnp.concatenate([part[:, width * j + NOPE : width * (j + 1)] for j in range(hd)], axis=1)
+    a_send[...] = nope.astype(BF16)
+    for k in range(nr):
+        ar_send[k] = rope[k * sd : (k + 1) * sd, :]
+    pl.semaphore_wait(barrier, len(pairs))
+    copies = []
+    for dr in order[:-1]:
+        copies.append(send(a_send, a_recv.at[dr - 1], a_ss.at[dr], a_rs.at[dr], dr, 0))
+    for dr in order[:-1]:
+        copies.append(
+            send(ar_send.at[lax.rem(r + dr, nr)], ar_recv.at[dr - 1], ar_ss.at[dr], ar_rs.at[dr], dr, 0)
+        )
+    n_own = [lens[slot[r * sd + i]] for i in range(sd)]
+    half = ROPE // 2
+    ld_freq.wait()
+    seq_of = lax.rem(iota((rows, half), 0), sd)
+    pos = jnp.zeros((rows, half), jnp.int32)
+    for i in range(sd):
+        pos = jnp.where(seq_of == i, n_own[i] - 1, pos)
+    angles = pos.astype(F32) * freq[...]
+    cosine = jnp.cos(angles)
+    sine = jnp.sin(angles)
+    rope_own = ar_send[r]
+    ld_wl.wait()
+    for c in copies:
+        c.wait_recv()
+    for k in range(nr - 1):
+        nope = nope + a_recv[k].astype(F32)
+        rope_own = rope_own + ar_recv[k]
+
+    turned = jnp.concatenate([rope_own[:, ROPE * j : ROPE * (j + 1)] for j in range(hd)], axis=0)
+    first, second = turned[:, :half], turned[:, half:]
+    turned = jnp.concatenate(
+        [first * cosine - second * sine, first * sine + second * cosine, jnp.zeros((rows, 128 - ROPE), F32)],
+        axis=1,
+    ).astype(BF16)
+    br_send[...] = turned
+    br_recv[h] = turned
+    nope = nope.astype(BF16)
+    absorbed = [
+        dot_nt(nope[:, NOPE * j : NOPE * (j + 1)], wl[:, (NOPE + V) * j : (NOPE + V) * j + NOPE])
+        for j in range(hd)
+    ]
+    for k in range(nr):
+        b_send[k] = jnp.concatenate([x[k * sd : (k + 1) * sd] for x in absorbed], axis=0).astype(BF16)
+    copies = []
+    for k, (dr, dh) in enumerate(pairs):
+        copies.append(
+            send(b_send.at[lax.rem(r + dr, nr)], b_recv.at[r, h], b_ss.at[k], b_rs.at[k], dr, dh)
+        )
+    for dh in range(1, nh):
+        copies.append(send(br_send, br_recv.at[h], br_ss.at[dh], br_rs.at[dh], 0, dh))
+    b_recv[r, h] = b_send[r]
+    ld_cl.wait()
+    ld_cr.wait()
+    total_rows = nh * rows
+    lane_pos = iota((total_rows, seg), 1) + h * seg
+    row_seq = lax.rem(iota((total_rows, seg), 0), sd)
+    limit = jnp.zeros((total_rows, seg), jnp.int32)
+    for i in range(sd):
+        limit = jnp.where(row_seq == i, n_own[i], limit)
+    in_range = lane_pos < limit
+    for c in copies:
+        c.wait_recv()
+
+    query = jnp.concatenate(
+        [
+            jnp.concatenate([b_recv[k, g] for g in range(nh)], axis=0)
+            for k in range(nr)
+        ],
+        axis=1,
+    )
+    query_rope = jnp.concatenate([br_recv[g] for g in range(nh)], axis=0)[:, :ROPE]
+    scores = jnp.zeros((total_rows, seg), F32)
+    for i in range(sd):
+        s_i = dot_nt(query, cl[i]) + dot_nn(query_rope, cr[i])
+        scores = jnp.where(row_seq == i, s_i, scores)
+    scores = jnp.where(in_range, scores * np.float32(1.0 / np.sqrt(NOPE + ROPE)), neg_big)
+    peak = jnp.max(scores, axis=1, keepdims=True)
+    weights = jnp.where(in_range, jnp.exp(scores - peak), 0.0)
+    summed = jnp.sum(weights, axis=1, keepdims=True)
+    diag = iota((total_rows, 128), 0) == iota((total_rows, 128), 1)
+    peak_row = jnp.sum(jnp.where(diag, peak, 0.0), axis=0, keepdims=True)
+    sum_row = jnp.sum(jnp.where(diag, summed, 0.0), axis=0, keepdims=True)
+    stat = jnp.where(iota((8, 128), 0) == 0, peak_row, sum_row)
+    st_send[...] = stat
+    copies = [
+        send(st_send, st_recv.at[dh - 1], st_ss.at[dh], st_rs.at[dh], 0, dh) for dh in range(1, nh)
+    ]
+    weights = weights.astype(BF16)
+    acc = jnp.zeros((total_rows, LAT), F32)
+    out_seq = lax.rem(iota((total_rows, LAT), 0), sd)
+    for i in range(sd):
+        acc = jnp.where(out_seq == i, dot_nn(weights, cl[i]), acc)
+    for c in copies:
+        c.wait_recv()
+    peaks = [peak_row] + [st_recv[k, 0:1, :] for k in range(nh - 1)]
+    sums = [sum_row] + [st_recv[k, 1:2, :] for k in range(nh - 1)]
+    top = functools.reduce(jnp.maximum, peaks)
+    total = functools.reduce(jnp.add, [s * jnp.exp(p - top) for p, s in zip(peaks, sums)])
+    lane_ok = iota((1, 128), 1) < total_rows
+    factor_row = jnp.where(lane_ok, jnp.exp(peak_row - top) / jnp.where(lane_ok, total, 1.0), 0.0)
+    factor = jnp.sum(jnp.where(diag, factor_row, 0.0), axis=1, keepdims=True)
+    acc = (acc * factor).astype(BF16)
+    for g in range(nh):
+        for k in range(nr):
+            d_send[k, g] = acc[g * rows : (g + 1) * rows, k * lb : (k + 1) * lb]
+    copies = []
+    for k, (dr, dh) in enumerate(pairs):
+        copies.append(
+            send(
+                d_send.at[lax.rem(r + dr, nr), lax.rem(h + dh, nh)],
+                d_recv.at[r, h], d_ss.at[k], d_rs.at[k], dr, dh,
+            )
+        )
+    d_recv[r, h] = d_send[r, h]
+    for c in copies:
+        c.wait_recv()
+
+    latent = [
+        functools.reduce(jnp.add, [d_recv[k, g].astype(F32) for g in range(nh)]) for k in range(nr)
+    ]
+    context = jnp.concatenate(
+        [
+            dot_nn(
+                jnp.concatenate([x[sd * j : sd * (j + 1)] for x in latent], axis=0).astype(BF16),
+                wl[:, (NOPE + V) * j + NOPE : (NOPE + V) * (j + 1)],
+            )
+            for j in range(hd)
+        ],
+        axis=1,
+    )
+    e_send[...] = context.astype(BF16)
+    copies = [
+        send(e_send, e_recv.at[dr - 1], e_ss.at[dr], e_rs.at[dr], dr, 0) for dr in order[:-1]
+    ]
+    ld_wo.wait()
+    for c in copies:
+        c.wait_recv()
+    for k in range(nr - 1):
+        context = context + e_recv[k].astype(F32)
+    out_part = dot_nt(context.astype(BF16), wo[...])
+    for k in range(nr):
+        f_send[k] = out_part[k * sd : (k + 1) * sd, :]
+
+    def final(k, slot_at):
+        return pltpu.make_async_remote_copy(
+            src_ref=f_send.at[k], dst_ref=f_recv.at[slot_at],
+            send_sem=f_ss.at[k], recv_sem=f_rs.at[slot_at],
+            device_id={"row": k, "head": r}, device_id_type=MESH,
+        )
+
+    for k in range(nr):
+        mine = jnp.logical_and(r == k, h == r)
+
+        @pl.when(jnp.logical_not(mine))
+        def _():
+            final(k, h).start()
+
+        @pl.when(mine)
+        def _():
+            f_recv[h] = f_send[k]
+
+    for c in pending:
+        c.wait_send()
+    for g in range(nh):
+
+        @pl.when(jnp.logical_not(jnp.logical_and(h == r, h == g)))
+        def _():
+            final(0, g).wait_recv()
+
+    out_ref[...] = functools.reduce(jnp.add, [f_recv[g] for g in range(nh)])
+    for k in range(nr):
+
+        @pl.when(jnp.logical_not(jnp.logical_and(r == k, h == r)))
+        def _():
+            final(k, h).wait_send()
+
+
+def local_fused(
+    nr, nh,
+    tokens, query_weight, latent_weight, output_weight, cache_latent, cache_rope, lengths, slot_seq
+):
+    sd, seg, _ = cache_latent.shape
+    hd = query_weight.shape[1] // (NOPE + ROPE)
+    batch = nr * sd
+    rows = sd * hd
+    lb = LAT // nr
+    db = query_weight.shape[0]
+    half = ROPE // 2
+    freq = np.power(10000.0, -2.0 * np.arange(half, dtype=np.float32) / ROPE).astype(np.float32)
+    vm = pltpu.VMEM
+    dma = pltpu.SemaphoreType.DMA
+    pairs = nr * nh - 1
+    scratch = [
+        vm((1, half), F32),
+        vm((batch, db), BF16),
+        vm(query_weight.shape, BF16),
+        vm(latent_weight.shape, BF16),
+        vm(output_weight.shape, BF16),
+        vm(cache_latent.shape, BF16),
+        vm(cache_rope.shape, BF16),
+        pltpu.SMEM(lengths.shape, jnp.int32),
+        pltpu.SMEM(slot_seq.shape, jnp.int32),
+        vm((batch, hd * NOPE), BF16),
+        vm((nr - 1, batch, hd * NOPE), BF16),
+        vm((nr, sd, hd * ROPE), F32),
+        vm((nr - 1, sd, hd * ROPE), F32),
+        vm((nr, rows, lb), BF16),
+        vm((nr, nh, rows, lb), BF16),
+        vm((rows, 128), BF16),
+        vm((nh, rows, 128), BF16),
+        vm((8, 128), F32),
+        vm((nh - 1, 8, 128), F32),
+        vm((nr, nh, rows, lb), BF16),
+        vm((nr, nh, rows, lb), BF16),
+        vm((batch, hd * V), BF16),
+        vm((nr - 1, batch, hd * V), BF16),
+        vm((nr, sd, db), F32),
+        vm((nh, sd, db), F32),
+        dma((9,)),
+    ]
+    for count in (nr, nr, pairs, nh, nh, pairs, nr, max(nr, nh)):
+        scratch += [dma((count,)), dma((count,))]
+    anywhere = pl.BlockSpec(memory_space=pl.ANY)
+    summed = pl.pallas_call(
+        functools.partial(fused, nr, nh, sd, hd),
+        out_shape=jax.ShapeDtypeStruct((sd, db), F32),
+        in_specs=[anywhere] * 9,
+        out_specs=pl.BlockSpec(memory_space=pltpu.VMEM),
+        scratch_shapes=scratch,
+        compiler_params=pltpu.CompilerParams(collective_id=0, has_side_effects=True),
+    )(
+        jnp.asarray(freq)[None, :], tokens, query_weight, latent_weight, output_weight,
+        cache_latent, cache_rope, lengths, slot_seq,
+    )
+    return summed.astype(BF16)
+
+
 def solution(mesh):
     placed = (
         P("groups", None),
@@ -159,6 +490,16 @@
         P("groups"),
         P("groups"),
     )
+    nr, nh = mesh.shape["row"], mesh.shape["head"]
+    square = nr == nh and nr > 1 and (LAT // nr) % 128 == 0
+
+    def choose(*args):
+        query_weight, cache_latent = args[1], args[4]
+        rows = cache_latent.shape[0] * (query_weight.shape[1] // (NOPE + ROPE))
+        if square and rows % 16 == 0 and rows * nh <= 128:
+            return local_fused(nr, nh, *args)
+        return local(*args)
+
     return jax.shard_map(
-        local, mesh=mesh, in_specs=placed, out_specs=P(("groups", "row"), "head"), check_vma=False
-    )
+        choose, mesh=mesh, in_specs=placed, out_specs=P(("groups", "row"), "head"), check_vma=False
+    )

time: 191 us -> 32.4 us (0.17)
  waiting for transfers between devices: 122 us -> 0 us
  Pallas kernels: 0 us -> 30.9 us
  blocking collectives: 22.9 us -> 0 us
  matrix products: 16.1 us -> 0 us
  between operations: 14 us -> 0.01 us
  local copies, waits for them, and re-layouts: 12.5 us -> 0 us
    all_gather x3 -> x0, waiting for transfers between devices: 98.1 us -> none  [the longest x1 58.2 us: local(): lax.all_gather(query_weight, 'row', axis=0, tiled=True)]
    pallas_call x0 -> x1, Pallas kernels: none -> 30.9 us  [local_fused(): pl.pallas_call(functools.partial(fused, nr, nh, sd, hd), out_shape=jax.Sh...]
    unnamed x5 -> x0, waiting for transfers between devices: 23.8 us -> none
    all_gather x4 -> x0, blocking collectives: 22.9 us -> none  [the longest x3 17.6 us: combined_all(): gathered = jax.tree.map(lambda a: lax.all_gather(a, axis), part)]
    dot_general x9 -> x0, matrix products: 16.1 us -> none  [the longest x1 7.3 us: local(): jnp.einsum('bhl,dhl->bd', own_heads, out_abs.reshape(D, heads_dev, LAT),...]
    unnamed x12 -> x0, local copies, waits for them, and re-layouts: 7.88 us -> none
    slice x4 -> x0, local copies, waits for them, and re-layouts: 2.35 us -> none  [the longest x1 2.32 us: absorb(): query_heads[:, :, NOPE:]]
  transfers between devices with their start and end apart: 4 -> 0, of which waited for: 4 -> 0; matrix products, arithmetic and copies ran while one was open for 10% -> 0% of each run, Pallas kernels for 0% -> 0%
where the time goes in v1:
time: 32.4 us; the launch traced here: 32.2 us
  Pallas kernels  30.9 us (95%)
  other arithmetic  1.29 us (4%)
    pallas_call x1, Pallas kernels, local_fused(): pl.pallas_call(functools.partial(fused, nr, nh, sd, hd), out_shape=jax.Sh...  30.9 us
    convert_element_type x1, other arithmetic, local_fused(): return summed.astype(BF16)  1.29 us

profile of v1, /device:TPU:0, one launch (start us, length us, event | category | flops | bytes accessed | tf_op | source)
XLA Modules:
  0.0 32.2 jit_solution(8165968712779834950)
XLA Ops:
  0.0 30.9 %shard_map.91 = f32[4,512]{1,0:T(4,128)} custom-call(f32[1,32]{1,0:T(1,128)} %constant.5.freq_h, bf16[16,2048]{1,0:T(8,128)(2,1)} %tok_h.1, bf16[512,768]{1,0:T(8,128)(2,1)} %wq_h.1, bf16[128,1024]{1,0:T(8,128)(2,1)} %wl_h.1, bf16[512,512]{1,0:T(8,128)(2,1)} %wo_h.1, bf16[4,512,512]{2,1,0:T(8,128)(2,1)} %cl_h.1, bf16[4,64,512]{2,1,0:T(8,128)(2,1)} %cr_h.1, ...), custom_call_target="tpu_custom_call" | custom-call | tf_op jit(solution)/shard_map/pallas_call | solution.py:468
  30.9 1.3 %convert_element_type.3 = bf16[4,512]{1,0:T(4,128)(2,1)} convert(f32[4,512]{1,0:T(4,128)} %shard_map.91) | non-fusion elementwise | flops 2048 | bytes 12288 | tf_op jit(solution)/shard_map/convert_element_type | solution.py:479

commit v2 on v1

--- a/solution.py
+++ b/solution.py
@@ -180,8 +180,7 @@
     st_send, st_recv, d_send, d_recv,
     e_send, e_recv, f_send, f_recv,
     load_sem,
-    a_ss, a_rs, ar_ss, ar_rs, b_ss, b_rs, br_ss, br_rs,
-    st_ss, st_rs, d_ss, d_rs, e_ss, e_rs, f_ss, f_rs,
+    send_sem, recv_sem,
 ):
     r = lax.axis_index("row")
     h = lax.axis_index("head")
@@ -215,17 +214,27 @@
             device_id={"row": lax.rem(r + dr, nr), "head": lax.rem(h + dh, nh)},
             device_id_type=MESH,
         )
-    pending = []
-
-    def send(src, dst, ss, rs, dr, dh):
-        c = pltpu.make_async_remote_copy(
-            src_ref=src, dst_ref=dst, send_sem=ss, recv_sem=rs,
+
+    def send(phase, src, dst, dr, dh):
+        pltpu.make_async_remote_copy(
+            src_ref=src, dst_ref=dst, send_sem=send_sem.at[phase], recv_sem=recv_sem.at[phase],
             device_id={"row": lax.rem(r + dr, nr), "head": lax.rem(h + dh, nh)},
             device_id_type=MESH,
-        )
-        c.start()
-        pending.append(c)
-        return c
+        ).start()
+
+    def span(phase, ref, count):
+        return pltpu.make_async_remote_copy(
+            src_ref=ref.at[pl.ds(0, count)], dst_ref=ref.at[pl.ds(0, count)],
+            send_sem=send_sem.at[phase], recv_sem=recv_sem.at[phase],
+            device_id={"row": lax.rem(r + 1, nr)}, device_id_type=MESH,
+        )
+
+    phases = [
+        span(0, a_recv, nr - 1), span(1, ar_recv, nr - 1), span(2, b_recv, nr * nh - 1),
+        span(3, br_recv, nh - 1), span(4, st_recv, nr * nh - 1), span(5, d_recv, nr * nh - 1),
+        span(6, e_recv, nr - 1),
+    ]
+    me = r * nh + h
 
     ld_slot.wait()
     ld_len.wait()
@@ -245,13 +254,10 @@
     for k in range(nr):
         ar_send[k] = rope[k * sd : (k + 1) * sd, :]
     pl.semaphore_wait(barrier, len(pairs))
-    copies = []
     for dr in order[:-1]:
-        copies.append(send(a_send, a_recv.at[dr - 1], a_ss.at[dr], a_rs.at[dr], dr, 0))
+        send(0, a_send, a_recv.at[dr - 1], dr, 0)
     for dr in order[:-1]:
-        copies.append(
-            send(ar_send.at[lax.rem(r + dr, nr)], ar_recv.at[dr - 1], ar_ss.at[dr], ar_rs.at[dr], dr, 0)
-        )
+        send(1, ar_send.at[lax.rem(r + dr, nr)], ar_recv.at[dr - 1], dr, 0)
     n_own = [lens[slot[r * sd + i]] for i in range(sd)]
     half = ROPE // 2
     ld_freq.wait()
@@ -262,14 +268,24 @@
     angles = pos.astype(F32) * freq[...]
     cosine = jnp.cos(angles)
     sine = jnp.sin(angles)
-    rope_own = ar_send[r]
     ld_wl.wait()
-    for c in copies:
-        c.wait_recv()
+    phases[0].wait_recv()
     for k in range(nr - 1):
         nope = nope + a_recv[k].astype(F32)
+
+    nope = nope.astype(BF16)
+    absorbed = [
+        dot_nt(nope[:, NOPE * j : NOPE * (j + 1)], wl[:, (NOPE + V) * j : (NOPE + V) * j + NOPE])
+        for j in range(hd)
+    ]
+    for k in range(nr):
+        b_send[k] = jnp.concatenate([x[k * sd : (k + 1) * sd] for x in absorbed], axis=0).astype(BF16)
+    for dr, dh in pairs:
+        send(2, b_send.at[lax.rem(r + dr, nr)], b_recv.at[me], dr, dh)
+    phases[1].wait_recv()
+    rope_own = ar_send[r]
+    for k in range(nr - 1):
         rope_own = rope_own + ar_recv[k]
-
     turned = jnp.concatenate([rope_own[:, ROPE * j : ROPE * (j + 1)] for j in range(hd)], axis=0)
     first, second = turned[:, :half], turned[:, half:]
     turned = jnp.concatenate(
@@ -278,21 +294,9 @@
     ).astype(BF16)
     br_send[...] = turned
     br_recv[h] = turned
-    nope = nope.astype(BF16)
-    absorbed = [
-        dot_nt(nope[:, NOPE * j : NOPE * (j + 1)], wl[:, (NOPE + V) * j : (NOPE + V) * j + NOPE])
-        for j in range(hd)
-    ]
-    for k in range(nr):
-        b_send[k] = jnp.concatenate([x[k * sd : (k + 1) * sd] for x in absorbed], axis=0).astype(BF16)
-    copies = []
-    for k, (dr, dh) in enumerate(pairs):
-        copies.append(
-            send(b_send.at[lax.rem(r + dr, nr)], b_recv.at[r, h], b_ss.at[k], b_rs.at[k], dr, dh)
-        )
     for dh in range(1, nh):
-        copies.append(send(br_send, br_recv.at[h], br_ss.at[dh], br_rs.at[dh], 0, dh))
-    b_recv[r, h] = b_send[r]
+        send(3, br_send, br_recv.at[h], 0, dh)
+    b_recv[me] = b_send[r]
     ld_cl.wait()
     ld_cr.wait()
     total_rows = nh * rows
@@ -302,12 +306,12 @@
     for i in range(sd):
         limit = jnp.where(row_seq == i, n_own[i], limit)
     in_range = lane_pos < limit
-    for c in copies:
-        c.wait_recv()
+    phases[2].wait_recv()
+    phases[3].wait_recv()
 
     query = jnp.concatenate(
         [
-            jnp.concatenate([b_recv[k, g] for g in range(nh)], axis=0)
+            jnp.concatenate([b_recv[k * nh + g] for g in range(nh)], axis=0)
             for k in range(nr)
         ],
         axis=1,
@@ -324,43 +328,48 @@
     diag = iota((total_rows, 128), 0) == iota((total_rows, 128), 1)
     peak_row = jnp.sum(jnp.where(diag, peak, 0.0), axis=0, keepdims=True)
     sum_row = jnp.sum(jnp.where(diag, summed, 0.0), axis=0, keepdims=True)
-    stat = jnp.where(iota((8, 128), 0) == 0, peak_row, sum_row)
+    stat = jnp.concatenate([peak_row, sum_row], axis=0)
     st_send[...] = stat
-    copies = [
-        send(st_send, st_recv.at[dh - 1], st_ss.at[dh], st_rs.at[dh], 0, dh) for dh in range(1, nh)
-    ]
+    for dr, dh in pairs:
+        send(4, st_send, st_recv.at[me], dr, dh)
+    st_recv[me] = stat
     weights = weights.astype(BF16)
     acc = jnp.zeros((total_rows, LAT), F32)
     out_seq = lax.rem(iota((total_rows, LAT), 0), sd)
     for i in range(sd):
         acc = jnp.where(out_seq == i, dot_nn(weights, cl[i]), acc)
-    for c in copies:
-        c.wait_recv()
-    peaks = [peak_row] + [st_recv[k, 0:1, :] for k in range(nh - 1)]
-    sums = [sum_row] + [st_recv[k, 1:2, :] for k in range(nh - 1)]
-    top = functools.reduce(jnp.maximum, peaks)
-    total = functools.reduce(jnp.add, [s * jnp.exp(p - top) for p, s in zip(peaks, sums)])
-    lane_ok = iota((1, 128), 1) < total_rows
-    factor_row = jnp.where(lane_ok, jnp.exp(peak_row - top) / jnp.where(lane_ok, total, 1.0), 0.0)
-    factor = jnp.sum(jnp.where(diag, factor_row, 0.0), axis=1, keepdims=True)
-    acc = (acc * factor).astype(BF16)
+    acc = acc.astype(BF16)
     for g in range(nh):
         for k in range(nr):
             d_send[k, g] = acc[g * rows : (g + 1) * rows, k * lb : (k + 1) * lb]
-    copies = []
-    for k, (dr, dh) in enumerate(pairs):
-        copies.append(
-            send(
-                d_send.at[lax.rem(r + dr, nr), lax.rem(h + dh, nh)],
-                d_recv.at[r, h], d_ss.at[k], d_rs.at[k], dr, dh,
-            )
-        )
-    d_recv[r, h] = d_send[r, h]
-    for c in copies:
-        c.wait_recv()
+    for dr, dh in pairs:
+        send(5, d_send.at[lax.rem(r + dr, nr), lax.rem(h + dh, nh)], d_recv.at[me], dr, dh)
+    d_recv[me] = d_send[r, h]
+    phases[4].wait_recv()
+    own_lane = iota((rows, 128), 1) == iota((rows, 128), 0) + h * rows
+    lane_ok = iota((1, 128), 1) < total_rows
+    factors = []
+    for k in range(nr):
+        peaks = [st_recv[k * nh + g, 0:1, :] for g in range(nh)]
+        top = functools.reduce(jnp.maximum, peaks)
+        scales = [jnp.exp(p - top) for p in peaks]
+        total = functools.reduce(
+            jnp.add, [st_recv[k * nh + g, 1:2, :] * scales[g] for g in range(nh)]
+        )
+        inverse = 1.0 / jnp.where(lane_ok, total, 1.0)
+        factors.append(
+            [
+                jnp.sum(jnp.where(own_lane, x * inverse, 0.0), axis=1, keepdims=True)
+                for x in scales
+            ]
+        )
+    phases[5].wait_recv()
 
     latent = [
-        functools.reduce(jnp.add, [d_recv[k, g].astype(F32) for g in range(nh)]) for k in range(nr)
+        functools.reduce(
+            jnp.add, [d_recv[k * nh + g].astype(F32) * factors[k][g] for g in range(nh)]
+        )
+        for k in range(nr)
     ]
     context = jnp.concatenate(
         [
@@ -373,50 +382,51 @@
         axis=1,
     )
     e_send[...] = context.astype(BF16)
-    copies = [
-        send(e_send, e_recv.at[dr - 1], e_ss.at[dr], e_rs.at[dr], dr, 0) for dr in order[:-1]
-    ]
+    for dr in order[:-1]:
+        send(6, e_send, e_recv.at[dr - 1], dr, 0)
     ld_wo.wait()
-    for c in copies:
-        c.wait_recv()
+    phases[6].wait_recv()
     for k in range(nr - 1):
         context = context + e_recv[k].astype(F32)
     out_part = dot_nt(context.astype(BF16), wo[...])
     for k in range(nr):
-        f_send[k] = out_part[k * sd : (k + 1) * sd, :]
-
-    def final(k, slot_at):
-        return pltpu.make_async_remote_copy(
-            src_ref=f_send.at[k], dst_ref=f_recv.at[slot_at],
-            send_sem=f_ss.at[k], recv_sem=f_rs.at[slot_at],
-            device_id={"row": k, "head": r}, device_id_type=MESH,
-        )
+        f_send[k] = out_part[k * sd : (k + 1) * sd, :].astype(BF16)
 
     for k in range(nr):
         mine = jnp.logical_and(r == k, h == r)
 
         @pl.when(jnp.logical_not(mine))
         def _():
-            final(k, h).start()
+            pltpu.make_async_remote_copy(
+                src_ref=f_send.at[k], dst_ref=f_recv.at[h],
+                send_sem=send_sem.at[7], recv_sem=recv_sem.at[7],
+                device_id={"row": k, "head": r}, device_id_type=MESH,
+            ).start()
 
         @pl.when(mine)
         def _():
             f_recv[h] = f_send[k]
 
-    for c in pending:
+    for c in phases:
         c.wait_send()
-    for g in range(nh):
-
-        @pl.when(jnp.logical_not(jnp.logical_and(h == r, h == g)))
-        def _():
-            final(0, g).wait_recv()
-
-    out_ref[...] = functools.reduce(jnp.add, [f_recv[g] for g in range(nh)])
-    for k in range(nr):
-
-        @pl.when(jnp.logical_not(jnp.logical_and(r == k, h == r)))
-        def _():
-            final(k, h).wait_send()
+
+    @pl.when(h == r)
+    def _():
+        span(7, f_recv, nh - 1).wait_recv()
+
+    @pl.when(h != r)
+    def _():
+        span(7, f_recv, nh).wait_recv()
+
+    out_ref[...] = functools.reduce(jnp.add, [f_recv[g].astype(F32) for g in range(nh)])
+
+    @pl.when(h == r)
+    def _():
+        span(7, f_send, nr - 1).wait_send()
+
+    @pl.when(h != r)
+    def _():
+        span(7, f_send, nr).wait_send()
 
 
 def local_fused(
@@ -433,7 +443,6 @@
     freq = np.power(10000.0, -2.0 * np.arange(half, dtype=np.float32) / ROPE).astype(np.float32)
     vm = pltpu.VMEM
     dma = pltpu.SemaphoreType.DMA
-    pairs = nr * nh - 1
     scratch = [
         vm((1, half), F32),
         vm((batch, db), BF16),
@@ -449,25 +458,25 @@
         vm((nr, sd, hd * ROPE), F32),
         vm((nr - 1, sd, hd * ROPE), F32),
         vm((nr, rows, lb), BF16),
-        vm((nr, nh, rows, lb), BF16),
+        vm((nr * nh, rows, lb), BF16),
         vm((rows, 128), BF16),
         vm((nh, rows, 128), BF16),
-        vm((8, 128), F32),
-        vm((nh - 1, 8, 128), F32),
+        vm((2, 128), F32),
+        vm((nr * nh, 2, 128), F32),
         vm((nr, nh, rows, lb), BF16),
-        vm((nr, nh, rows, lb), BF16),
+        vm((nr * nh, rows, lb), BF16),
         vm((batch, hd * V), BF16),
         vm((nr - 1, batch, hd * V), BF16),
-        vm((nr, sd, db), F32),
-        vm((nh, sd, db), F32),
+        vm((nr, sd, db), BF16),
+        vm((nh, sd, db), BF16),
         dma((9,)),
+        dma((8,)),
+        dma((8,)),
     ]
-    for count in (nr, nr, pairs, nh, nh, pairs, nr, max(nr, nh)):
-        scratch += [dma((count,)), dma((count,))]
     anywhere = pl.BlockSpec(memory_space=pl.ANY)
     summed = pl.pallas_call(
         functools.partial(fused, nr, nh, sd, hd),
-        out_shape=jax.ShapeDtypeStruct((sd, db), F32),
+        out_shape=pltpu.VMEM((sd, db), F32),
         in_specs=[anywhere] * 9,
         out_specs=pl.BlockSpec(memory_space=pltpu.VMEM),
         scratch_shapes=scratch,

time: 32.4 us -> 27.5 us (0.85)
  Pallas kernels: 30.9 us -> 26.8 us
  other arithmetic: 1.29 us -> 0.6 us
    pallas_call x1, Pallas kernels: 30.9 us -> 26.8 us  [local_fused(): pl.pallas_call(functools.partial(fused, nr, nh, sd, hd), out_shape=pltpu....]
    convert_element_type x1, other arithmetic: 1.29 us -> 0.6 us  [local_fused(): return summed.astype(BF16)]
where the time goes in v2:
time: 27.5 us; the launch traced here: 27.4 us
  Pallas kernels  26.8 us (97%)
  other arithmetic  0.6 us (2%)
    pallas_call x1, Pallas kernels, local_fused(): pl.pallas_call(functools.partial(fused, nr, nh, sd, hd), out_shape=pltpu....  26.8 us
    convert_element_type x1, other arithmetic, local_fused(): return summed.astype(BF16)  0.6 us

profile of v2, /device:TPU:0, one launch (start us, length us, event | category | flops | bytes accessed | tf_op | source)
XLA Modules:
  0.0 27.4 jit_solution(8730475913288608916)
XLA Ops:
  0.0 26.8 %shard_map.91 = f32[4,512]{1,0:T(4,128)S(1)} custom-call(f32[1,32]{1,0:T(1,128)} %constant.5.freq_h, bf16[16,2048]{1,0:T(8,128)(2,1)} %tok_h.1, bf16[512,768]{1,0:T(8,128)(2,1)} %wq_h.1, bf16[128,1024]{1,0:T(8,128)(2,1)} %wl_h.1, bf16[512,512]{1,0:T(8,128)(2,1)} %wo_h.1, bf16[4,512,512]{2,1,0:T(8,128)(2,1)} %cl_h.1, bf16[4,64,512]{2,1,0:T(8,128)(2,1)} %cr_h.1, ...), custom_call_target="tpu_custom_call" | custom-call | tf_op jit(solution)/shard_map/pallas_call | solution.py:477
  26.8 0.6 %convert_element_type.3 = bf16[4,512]{1,0:T(4,128)(2,1)} convert(f32[4,512]{1,0:T(4,128)S(1)} %shard_map.91) | non-fusion elementwise | flops 2048 | bytes 12288 | tf_op jit(solution)/shard_map/convert_element_type | solution.py:488

commit v3 on v2

--- a/solution.py
+++ b/solution.py
@@ -171,10 +171,10 @@
 
 
 def fused(
-    nr, nh, sd, hd,
+    ng, nr, nh, sd, hd,
     freq_h, tok_h, wq_h, wl_h, wo_h, cl_h, cr_h, len_h, slot_h,
     out_ref,
-    freq, tok, wq, wl, wo, cl, cr, lens, slot,
+    freq, tok, wq, wl, wo, cl, cr, lens, slot, wv,
     a_send, a_recv, ar_send, ar_recv,
     b_send, b_recv, br_send, br_recv,
     st_send, st_recv, d_send, d_recv,
@@ -184,6 +184,8 @@
 ):
     r = lax.axis_index("row")
     h = lax.axis_index("head")
+    grp = lax.axis_index("groups")
+    share = hd // ng
     batch = nr * sd
     rows = sd * hd
     db = wq.shape[0]
@@ -201,6 +203,9 @@
     ld_wq = load(3, wq_h, wq)
     ld_freq = load(4, freq_h, freq)
     ld_wl = load(5, wl_h, wl)
+    ld_wv = [
+        load(9 + j, wl_h.at[:, pl.ds((NOPE + V) * j + NOPE, V)], wv.at[j, r]) for j in range(hd)
+    ]
     ld_cl = load(6, cl_h, cl)
     ld_cr = load(7, cr_h, cr)
     ld_wo = load(8, wo_h, wo)
@@ -215,6 +220,11 @@
             device_id_type=MESH,
         )
 
+    for dg in range(1, ng):
+        pl.semaphore_signal(
+            barrier, inc=1, device_id={"groups": lax.rem(grp + dg, ng)}, device_id_type=MESH
+        )
+
     def send(phase, src, dst, dr, dh):
         pltpu.make_async_remote_copy(
             src_ref=src, dst_ref=dst, send_sem=send_sem.at[phase], recv_sem=recv_sem.at[phase],
@@ -231,10 +241,31 @@
 
     phases = [
         span(0, a_recv, nr - 1), span(1, ar_recv, nr - 1), span(2, b_recv, nr * nh - 1),
-        span(3, br_recv, nh - 1), span(4, st_recv, nr * nh - 1), span(5, d_recv, nr * nh - 1),
+        span(3, br_recv, nh - 1), span(4, st_recv, nh - 1), span(5, d_recv, nh - 1),
         span(6, e_recv, nr - 1),
     ]
     me = r * nh + h
+
+    def spread(p):
+        j = grp * share + p
+        for dr in order[:-1]:
+            send(8 + p, wv.at[j, r], wv.at[j, r], dr, 0)
+
+    def swap(p):
+        j = grp * share + p
+        span(8 + p, wv.at[0], nr - 1).wait_recv()
+        for dg in range(1, ng):
+            for dr in order[:-1]:
+                k = lax.rem(r + dr, nr)
+                pltpu.make_async_remote_copy(
+                    src_ref=wv.at[j, k], dst_ref=wv.at[j, k],
+                    send_sem=send_sem.at[8 + share + p], recv_sem=recv_sem.at[8 + share + p],
+                    device_id={"groups": lax.rem(grp + dg, ng)}, device_id_type=MESH,
+                ).start()
+
+    for p in range(share):
+        phases.append(span(8 + p, wv.at[0], nr - 1))
+        phases.append(span(8 + share + p, wv.at[0], nr - 1))
 
     ld_slot.wait()
     ld_len.wait()
@@ -253,11 +284,14 @@
     a_send[...] = nope.astype(BF16)
     for k in range(nr):
         ar_send[k] = rope[k * sd : (k + 1) * sd, :]
-    pl.semaphore_wait(barrier, len(pairs))
+    for x in ld_wv:
+        x.wait()
+    pl.semaphore_wait(barrier, len(pairs) + ng - 1)
     for dr in order[:-1]:
         send(0, a_send, a_recv.at[dr - 1], dr, 0)
     for dr in order[:-1]:
         send(1, ar_send.at[lax.rem(r + dr, nr)], ar_recv.at[dr - 1], dr, 0)
+    spread(0)
     n_own = [lens[slot[r * sd + i]] for i in range(sd)]
     half = ROPE // 2
     ld_freq.wait()
@@ -296,6 +330,9 @@
     br_recv[h] = turned
     for dh in range(1, nh):
         send(3, br_send, br_recv.at[h], 0, dh)
+    for p in range(1, share):
+        spread(p)
+    swap(0)
     b_recv[me] = b_send[r]
     ld_cl.wait()
     ld_cr.wait()
@@ -330,9 +367,9 @@
     sum_row = jnp.sum(jnp.where(diag, summed, 0.0), axis=0, keepdims=True)
     stat = jnp.concatenate([peak_row, sum_row], axis=0)
     st_send[...] = stat
-    for dr, dh in pairs:
-        send(4, st_send, st_recv.at[me], dr, dh)
-    st_recv[me] = stat
+    for dh in range(1, nh):
+        send(4, st_send, st_recv.at[h], 0, dh)
+    st_recv[h] = stat
     weights = weights.astype(BF16)
     acc = jnp.zeros((total_rows, LAT), F32)
     out_seq = lax.rem(iota((total_rows, LAT), 0), sd)
@@ -340,54 +377,44 @@
         acc = jnp.where(out_seq == i, dot_nn(weights, cl[i]), acc)
     acc = acc.astype(BF16)
     for g in range(nh):
-        for k in range(nr):
-            d_send[k, g] = acc[g * rows : (g + 1) * rows, k * lb : (k + 1) * lb]
-    for dr, dh in pairs:
-        send(5, d_send.at[lax.rem(r + dr, nr), lax.rem(h + dh, nh)], d_recv.at[me], dr, dh)
-    d_recv[me] = d_send[r, h]
+        d_send[g] = acc[g * rows : (g + 1) * rows]
+    for dh in range(1, nh):
+        send(5, d_send.at[lax.rem(h + dh, nh)], d_recv.at[h], 0, dh)
+    d_recv[h] = d_send[h]
+    for p in range(1, share):
+        swap(p)
     phases[4].wait_recv()
     own_lane = iota((rows, 128), 1) == iota((rows, 128), 0) + h * rows
     lane_ok = iota((1, 128), 1) < total_rows
-    factors = []
-    for k in range(nr):
-        peaks = [st_recv[k * nh + g, 0:1, :] for g in range(nh)]
-        top = functools.reduce(jnp.maximum, peaks)
-        scales = [jnp.exp(p - top) for p in peaks]
-        total = functools.reduce(
-            jnp.add, [st_recv[k * nh + g, 1:2, :] * scales[g] for g in range(nh)]
-        )
-        inverse = 1.0 / jnp.where(lane_ok, total, 1.0)
-        factors.append(
-            [
-                jnp.sum(jnp.where(own_lane, x * inverse, 0.0), axis=1, keepdims=True)
-                for x in scales
-            ]
-        )
+    peaks = [st_recv[g, 0:1, :] for g in range(nh)]
+    top = functools.reduce(jnp.maximum, peaks)
+    scales = [jnp.exp(p - top) for p in peaks]
+    total = functools.reduce(jnp.add, [st_recv[g, 1:2, :] * scales[g] for g in range(nh)])
+    inverse = 1.0 / jnp.where(lane_ok, total, 1.0)
+    factors = [
+        jnp.sum(jnp.where(own_lane, x * inverse, 0.0), axis=1, keepdims=True) for x in scales
+    ]
     phases[5].wait_recv()
 
-    latent = [
-        functools.reduce(
-            jnp.add, [d_recv[k * nh + g].astype(F32) * factors[k][g] for g in range(nh)]
-        )
-        for k in range(nr)
-    ]
+    latent = functools.reduce(
+        jnp.add, [d_recv[g].astype(F32) * factors[g] for g in range(nh)]
+    )
+    for p in range(share):
+        span(8 + share + p, wv.at[0], nr - 1).wait_recv()
     context = jnp.concatenate(
         [
-            dot_nn(
-                jnp.concatenate([x[sd * j : sd * (j + 1)] for x in latent], axis=0).astype(BF16),
-                wl[:, (NOPE + V) * j + NOPE : (NOPE + V) * (j + 1)],
-            )
+            dot_nn(latent[sd * j : sd * (j + 1)].astype(BF16), wv[j].reshape(nr * lb, V))
             for j in range(hd)
         ],
         axis=1,
-    )
-    e_send[...] = context.astype(BF16)
+    ).astype(BF16)
+    e_send[...] = context
     for dr in order[:-1]:
-        send(6, e_send, e_recv.at[dr - 1], dr, 0)
+        send(6, e_send, e_recv.at[r], dr, 0)
+    e_recv[r] = context
     ld_wo.wait()
     phases[6].wait_recv()
-    for k in range(nr - 1):
-        context = context + e_recv[k].astype(F32)
+    context = jnp.concatenate([e_recv[k].astype(F32) for k in range(nr)], axis=0)
     out_part = dot_nt(context.astype(BF16), wo[...])
     for k in range(nr):
         f_send[k] = out_part[k * sd : (k + 1) * sd, :].astype(BF16)
@@ -430,7 +457,7 @@
 
 
 def local_fused(
-    nr, nh,
+    ng, nr, nh,
     tokens, query_weight, latent_weight, output_weight, cache_latent, cache_rope, lengths, slot_seq
 ):
     sd, seg, _ = cache_latent.shape
@@ -441,6 +468,7 @@
     db = query_weight.shape[0]
     half = ROPE // 2
     freq = np.power(10000.0, -2.0 * np.arange(half, dtype=np.float32) / ROPE).astype(np.float32)
+    share = hd // ng
     vm = pltpu.VMEM
     dma = pltpu.SemaphoreType.DMA
     scratch = [
@@ -453,6 +481,7 @@
         vm(cache_rope.shape, BF16),
         pltpu.SMEM(lengths.shape, jnp.int32),
         pltpu.SMEM(slot_seq.shape, jnp.int32),
+        vm((hd, nr, lb, V), BF16),
         vm((batch, hd * NOPE), BF16),
         vm((nr - 1, batch, hd * NOPE), BF16),
         vm((nr, sd, hd * ROPE), F32),
@@ -462,20 +491,20 @@
         vm((rows, 128), BF16),
         vm((nh, rows, 128), BF16),
         vm((2, 128), F32),
-        vm((nr * nh, 2, 128), F32),
-        vm((nr, nh, rows, lb), BF16),
-        vm((nr * nh, rows, lb), BF16),
-        vm((batch, hd * V), BF16),
-        vm((nr - 1, batch, hd * V), BF16),
+        vm((nh, 2, 128), F32),
+        vm((nh, rows, LAT), BF16),
+        vm((nh, rows, LAT), BF16),
+        vm((sd, hd * V), BF16),
+        vm((nr, sd, hd * V), BF16),
         vm((nr, sd, db), BF16),
         vm((nh, sd, db), BF16),
-        dma((9,)),
-        dma((8,)),
-        dma((8,)),
+        dma((9 + hd,)),
+        dma((8 + 2 * share,)),
+        dma((8 + 2 * share,)),
     ]
     anywhere = pl.BlockSpec(memory_space=pl.ANY)
     summed = pl.pallas_call(
-        functools.partial(fused, nr, nh, sd, hd),
+        functools.partial(fused, ng, nr, nh, sd, hd),
         out_shape=pltpu.VMEM((sd, db), F32),
         in_specs=[anywhere] * 9,
         out_specs=pl.BlockSpec(memory_space=pltpu.VMEM),
@@ -499,14 +528,15 @@
         P("groups"),
         P("groups"),
     )
-    nr, nh = mesh.shape["row"], mesh.shape["head"]
-    square = nr == nh and nr > 1 and (LAT // nr) % 128 == 0
+    ng, nr, nh = (mesh.shape[a] for a in ("groups", "row", "head"))
+    square = ng == 2 and nr == nh and nr > 1 and (LAT // nr) % 128 == 0
 
     def choose(*args):
         query_weight, cache_latent = args[1], args[4]
-        rows = cache_latent.shape[0] * (query_weight.shape[1] // (NOPE + ROPE))
-        if square and rows % 16 == 0 and rows * nh <= 128:
-            return local_fused(nr, nh, *args)
+        hd = query_weight.shape[1] // (NOPE + ROPE)
+        rows = cache_latent.shape[0] * hd
+        if square and hd % ng == 0 and rows % 16 == 0 and rows * nh <= 128:
+            return local_fused(ng, nr, nh, *args)
         return local(*args)
 
     return jax.shard_map(

time: 27.5 us -> 30.1 us (1.095)
  Pallas kernels: 26.8 us -> 29.4 us
    pallas_call x1, Pallas kernels: 26.8 us -> 29.4 us  [local_fused(): pl.pallas_call(functools.partial(fused, ng, nr, nh, sd, hd), out_shape=pl...]
where the time goes in v3:
time: 30.1 us; the launch traced here: 30 us
  Pallas kernels  29.4 us (98%)
  other arithmetic  0.6 us (2%)
    pallas_call x1, Pallas kernels, local_fused(): pl.pallas_call(functools.partial(fused, ng, nr, nh, sd, hd), out_shape=pl...  29.4 us

profile of v3, /device:TPU:0, one launch (start us, length us, event | category | flops | bytes accessed | tf_op | source)
XLA Modules:
  0.0 30.0 jit_solution(8328063797039943727)
XLA Ops:
  0.0 29.4 %shard_map.91 = f32[4,512]{1,0:T(4,128)S(1)} custom-call(f32[1,32]{1,0:T(1,128)} %constant.5.freq_h, bf16[16,2048]{1,0:T(8,128)(2,1)} %tok_h.1, bf16[512,768]{1,0:T(8,128)(2,1)} %wq_h.1, bf16[128,1024]{1,0:T(8,128)(2,1)} %wl_h.1, bf16[512,512]{1,0:T(8,128)(2,1)} %wo_h.1, bf16[4,512,512]{2,1,0:T(8,128)(2,1)} %cl_h.1, bf16[4,64,512]{2,1,0:T(8,128)(2,1)} %cr_h.1, ...), custom_call_target="tpu_custom_call" | custom-call | tf_op jit(solution)/shard_map/pallas_call | solution.py:506
  29.4 0.6 %convert_element_type.3 = bf16[4,512]{1,0:T(4,128)(2,1)} convert(f32[4,512]{1,0:T(4,128)S(1)} %shard_map.91) | non-fusion elementwise | flops 2048 | bytes 12288 | tf_op jit(solution)/shard_map/convert_element_type | solution.py:517

commit v4 on v2

--- a/solution.py
+++ b/solution.py
@@ -205,8 +205,15 @@
     ld_cr = load(7, cr_h, cr)
     ld_wo = load(8, wo_h, wo)
 
-    order = [dr for dr in range(nr) if dr] + [0]
-    pairs = [(dr, dh) for dr in order for dh in range(nh) if dr or dh]
+    order = []
+    high = lax.div(2 * r, nr)
+    for k in range(nr - 1):
+        down = nr - 1 - k
+        down = down - 1 + lax.div(down - r + nr - 1, nr)
+        up = k + lax.div(k - r + nr, nr)
+        order.append(lax.rem((1 - high) * down + high * up - r + nr, nr))
+    order.append(0)
+    pairs = [(dr, dh) for dr in order for dh in range(nh) if dr is not order[-1] or dh]
     barrier = pltpu.get_barrier_semaphore()
     for dr, dh in pairs:
         pl.semaphore_signal(
@@ -333,12 +340,10 @@
     for dr, dh in pairs:
         send(4, st_send, st_recv.at[me], dr, dh)
     st_recv[me] = stat
-    weights = weights.astype(BF16)
-    acc = jnp.zeros((total_rows, LAT), F32)
-    out_seq = lax.rem(iota((total_rows, LAT), 0), sd)
-    for i in range(sd):
-        acc = jnp.where(out_seq == i, dot_nn(weights, cl[i]), acc)
-    acc = acc.astype(BF16)
+    spread = jnp.concatenate(
+        [jnp.where(row_seq == i, weights, 0.0).astype(BF16) for i in range(sd)], axis=1
+    )
+    acc = dot_nn(spread, cl[...].reshape(sd * seg, LAT)).astype(BF16)
     for g in range(nh):
         for k in range(nr):
             d_send[k, g] = acc[g * rows : (g + 1) * rows, k * lb : (k + 1) * lb]

time: 27.5 us -> 26.8 us (0.975)
  Pallas kernels: 26.8 us -> 26.1 us
    pallas_call x1, Pallas kernels: 26.8 us -> 26.1 us  [local_fused(): pl.pallas_call(functools.partial(fused, nr, nh, sd, hd), out_shape=pltpu....]
where the time goes in v4:
time: 26.8 us; the launch traced here: 26.7 us
  Pallas kernels  26.1 us (97%)
  other arithmetic  0.6 us (2%)
    pallas_call x1, Pallas kernels, local_fused(): pl.pallas_call(functools.partial(fused, nr, nh, sd, hd), out_shape=pltpu....  26.1 us
    convert_element_type x1, other arithmetic, local_fused(): return summed.astype(BF16)  0.6 us

profile of v4, /device:TPU:0, one launch (start us, length us, event | category | flops | bytes accessed | tf_op | source)
XLA Modules:
  0.0 26.7 jit_solution(1554207449318702807)
XLA Ops:
  0.0 26.1 %shard_map.91 = f32[4,512]{1,0:T(4,128)S(1)} custom-call(f32[1,32]{1,0:T(1,128)} %constant.5.freq_h, bf16[16,2048]{1,0:T(8,128)(2,1)} %tok_h.1, bf16[512,768]{1,0:T(8,128)(2,1)} %wq_h.1, bf16[128,1024]{1,0:T(8,128)(2,1)} %wl_h.1, bf16[512,512]{1,0:T(8,128)(2,1)} %wo_h.1, bf16[4,512,512]{2,1,0:T(8,128)(2,1)} %cl_h.1, bf16[4,64,512]{2,1,0:T(8,128)(2,1)} %cr_h.1, ...), custom_call_target="tpu_custom_call" | custom-call | tf_op jit(solution)/shard_map/pallas_call | solution.py:482
  26.1 0.6 %convert_element_type.3 = bf16[4,512]{1,0:T(4,128)(2,1)} convert(f32[4,512]{1,0:T(4,128)S(1)} %shard_map.91) | non-fusion elementwise | flops 2048 | bytes 12288 | tf_op jit(solution)/shard_map/convert_element_type | solution.py:493
